TPU v7x, 256 devices: a 4x2x16 block of a 4x16x16 slice. The times are simulated.
256 devices in a mesh: grp: 2 (over y), slab: 32 (over z, core), ang: 4 (over x).
Axes of the slice: x: 4, y: 2, z: 16, core: 2. Of those that a mesh axis runs over, the one named last changes fastest.
The devices are a block of a 4x16x16 slice.
Arguments:
- volume: bfloat16 [128, 256, 1024], P(('grp', 'slab')), parts along dimension 0, may hold values from -6 to 6
- ray_weights: bfloat16 [8, 1024, 1024], P('ang'), may hold values from -0.0234375 to 0.0234375
- row_offsets: int32 [8, 64], P('ang'), may hold values from 0 to 8
- measured: float32 [16, 256, 1024], P(('grp', 'ang'), 'slab'), parts along dimension 0, may hold values from -6 to 6
- shifts: float32 [16], P(('grp', 'ang')), parts along dimension 0, may hold values from -4 to 4
Outputs:
- updated_volume: bfloat16 [128, 256, 1024], P(('grp', 'slab')), parts along dimension 0
- last_residual: float32 [16, 256, 1024], P(('grp', 'ang'), 'slab'), parts along dimension 0
- shift_slope: float32 [16], P(('grp', 'ang')), parts along dimension 0
There are 2 independent parts, one for each index of `grp`. A program takes and returns all parts, laid end to end along the dimension named above; an argument that names none is the same for every part. Nothing has to cross between parts.
All inputs are finite; a program needn't handle non-finite values.
Results may differ from a plain program's by a relative error of at most 0.006.
Values may be sent and summed in bfloat16 or wider, within the bound.
No kernel may reach another device: no remote copies, remote signals or barrier semaphores. Data moves between devices by JAX's collectives and lax.ppermute only.
A program may use at most 128 MiB of HBM per device.

v0:
```python
import math
import jax
import jax.numpy as jnp
from jax import lax
from jax.sharding import Mesh
from jax.sharding import PartitionSpec as P

Y = 256
X = 1024
U = 1024
OFF = 8
ROUNDS = 2
SLAB = ("slab_0", "slab_1")
GRP_SLAB = ("grp", "slab_0", "slab_1")
step_size = 0.5


def own_block(tiles, axes, order):
    lengths = [lax.axis_size(a) for a in axes]
    tiles = tiles.reshape(*lengths, *tiles.shape[1:])
    tiles = tiles.transpose(*order, *range(len(axes), tiles.ndim))
    tiles = tiles.reshape(-1, *tiles.shape[len(axes) :])
    for k in order:
        tiles = lax.psum_scatter(tiles, axes[k], scatter_dimension=0, tiled=True)
    return tiles[0]


def in_blocks(shard, dim, length):
    lengths = shard.shape
    tiles = shard.reshape(*lengths[:dim], length, lengths[dim] // length, *lengths[dim + 1 :])
    return jnp.moveaxis(tiles, dim, 0)


def summed_rows(shard, axes, order, dim):
    length = lax.axis_size(axes)
    return own_block(in_blocks(shard, dim, length), axes, order)


def in_order(tiles, dim):
    lengths = list(tiles.shape[1:])
    lengths[dim] *= tiles.shape[0]
    return jnp.moveaxis(tiles, 0, dim).reshape(lengths)


def stacked_from(shard, axes, order):
    tiles = shard
    for k in order:
        tiles = lax.all_gather(tiles, axes[k])
    done = order[::-1]
    back = [done.index(k) for k in range(len(axes))]
    tiles = tiles.transpose(*back, *range(len(axes), tiles.ndim))
    return tiles.reshape(-1, *shard.shape)


def gather_axes(shard, axes, order, dim):
    return in_order(stacked_from(shard, axes, order), dim)


def from_everyone(shard, axis):
    copies = jnp.broadcast_to(shard, (lax.axis_size(axis), *shard.shape))
    return lax.all_to_all(copies, axis, split_axis=0, concat_axis=0, tiled=True)


def over_copies(shard, axis):
    return from_everyone(shard, axis).sum(axis=0)


def move_down(products, tilt_table):
    base = jnp.zeros((products.shape[1] + OFF, U), jnp.float32)
    placed = jax.vmap(
        lambda block, shift_rows: lax.dynamic_update_slice(base, block, (shift_rows, jnp.int32(0)))
    )(products, tilt_table)
    return jnp.sum(placed, axis=0)


def backproject(extended, tilt_table, ray_weights, band_rows):
    slices_count = tilt_table.shape[1]
    running = jnp.zeros((slices_count * band_rows, X), jnp.float32)
    for angle_index in range(ray_weights.shape[0]):
        source = extended[angle_index]
        picked = jax.vmap(
            lambda shift_rows: lax.dynamic_slice(source, (shift_rows, jnp.int32(0)), (band_rows, U))
        )(tilt_table[angle_index])
        running = running + lax.dot_general(
            picked.reshape(slices_count * band_rows, U),
            ray_weights[angle_index],
            (((1,), (1,)), ((), ())),
            preferred_element_type=jnp.float32,
        )
    return running


def apply_update(current, running):
    partial_value = lax.optimization_barrier(running.reshape(current.shape).astype(jnp.bfloat16))
    partial_wide = partial_value.astype(jnp.float32)
    gradient = lax.psum(partial_wide, "ang")
    renewed = (current.astype(jnp.float32) - step_size * gradient).astype(jnp.bfloat16)
    return renewed


def per_device(volume, ray_weights, row_offsets, measured, shifts):
    angles_here = ray_weights.shape[0]
    band_rows = measured.shape[1]
    highest = lax.Precision.HIGHEST
    numbers = lax.iota(jnp.int32, U)
    turns = numbers[:, None] * numbers[None, :] % U
    radians = turns.astype(jnp.float32) * (2.0 * math.pi / U)
    cosine = jnp.cos(radians)
    sine = jnp.sin(radians)
    signed = jnp.where(numbers <= (U - 1) // 2, numbers, numbers - U)
    omega = signed.astype(jnp.float32) * (2.0 * math.pi / U)
    flat_rows = measured.reshape(angles_here * band_rows, U)
    real_part = jnp.dot(flat_rows, cosine, precision=highest).reshape(angles_here, band_rows, U)
    imag_part = -jnp.dot(flat_rows, sine, precision=highest).reshape(angles_here, band_rows, U)
    phase = omega[None, None, :] * shifts[:, None, None]
    turned_real = real_part * jnp.cos(phase) + imag_part * jnp.sin(phase)
    turned_imag = imag_part * jnp.cos(phase) - real_part * jnp.sin(phase)
    first_half = jnp.concatenate([turned_real, omega * turned_imag], axis=0).reshape(-1, U)
    second_half = jnp.concatenate([turned_imag, -omega * turned_real], axis=0).reshape(-1, U)
    inverse = (
        jnp.dot(first_half, cosine, precision=highest)
        - jnp.dot(second_half, sine, precision=highest)
    ) / U
    inverse = inverse.reshape(2, angles_here, band_rows, U)
    shifted = inverse[0]
    slope_field = inverse[1]
    projection = shifted
    residual = shifted
    current = volume
    slices_here = volume.shape[0]
    tilt_table = lax.dynamic_slice_in_dim(
        row_offsets, lax.axis_index(SLAB) * slices_here, slices_here, 1
    )
    for round_index in range(ROUNDS):
        flattened = current.reshape(slices_here * Y, X)
        partials = jnp.stack(
            [
                move_down(
                    jnp.dot(
                        flattened, ray_weights[angle_index], preferred_element_type=jnp.float32
                    ).reshape(slices_here, Y, U),
                    tilt_table[angle_index],
                )[:Y]
                for angle_index in range(angles_here)
            ]
        )
        projection = summed_rows(partials, SLAB, (1, 0), 1)
        residual = projection - shifted
        rounded = residual.astype(jnp.bfloat16)
        gathered = gather_axes(rounded, SLAB, (0, 1), 1)
        extended = jnp.concatenate(
            [gathered, jnp.zeros((angles_here, OFF, U), jnp.bfloat16)], axis=1
        )
        running = backproject(extended, tilt_table, ray_weights, Y)
        current = apply_update(current, running)
    local_dot = jnp.sum(projection * slope_field, axis=(1, 2))
    shift_slope = over_copies(local_dot, SLAB) / math.sqrt(Y * U)
    return (current, residual, shift_slope)


def solution(mesh):
    split = Mesh(
        mesh.devices.reshape(mesh.shape["grp"], 16, 2, mesh.shape["ang"]),
        ("grp", "slab_0", "slab_1", "ang"),
    )
    placed = (
        P(GRP_SLAB, None, None),
        P("ang", None, None),
        P("ang", None),
        P(("grp", "ang"), SLAB, None),
        P(("grp", "ang")),
    )
    return jax.shard_map(
        per_device,
        mesh=split,
        in_specs=placed,
        out_specs=(P(GRP_SLAB, None, None), P(("grp", "ang"), SLAB, None), P(("grp", "ang"))),
        check_vma=False,
    )
```

profile of v0, /device:TPU:34, one launch (start us, length us, event | category | flops | bytes accessed | tf_op | source)
XLA Modules:
  0.0 536.4 jit_solution(7147799609888639398)
XLA Ops:
  7.3 4.7 fusion.16
  15.2 18.0 %while.12 = (s32[]{:T(128)}, f32[2,264,1024]{2,1,0:T(8,128)S(1)}, s32[2,3]{1,0:T(2,128)S(1)}, f32[2,256,1024]{2,1,0:T(8,128)}, s32[]{:T(128)}, /*index=5*/s32[3]{0:T(128)S(1)}, s32[]{:T(128)}) while((s32[]{:T(128)}, f32[2,264,1024]{2,1,0:T(8,128)S(1)}, s32[2,3]{1,0:T(2,128)S(1)}, f32[2,256,1024]{2,1,0:T(8,128)}, s32[]{:T(128)}, ...), condition=%wide.while_cond.4, body=%wide.while_body.4.sunk | while | flops 262163 | bytes 5243051 | solution.py:71
  18.7 3.4 dynamic-slice_select_fusion.8
  27.7 3.4 dynamic-slice_select_fusion.8
  34.9 24.1 %while.13 = (s32[]{:T(128)}, f32[2,264,1024]{2,1,0:T(8,128)}, s32[2,3]{1,0:T(2,128)S(1)}, f32[2,256,1024]{2,1,0:T(8,128)}, s32[]{:T(128)}, /*index=5*/s32[3]{0:T(128)S(1)}, s32[]{:T(128)}) while((s32[]{:T(128)}, f32[2,264,1024]{2,1,0:T(8,128)}, s32[2,3]{1,0:T(2,128)S(1)}, f32[2,256,1024]{2,1,0:T(8,128)}, s32[]{:T(128)}, /*index=5*/s32[3]{0:T(128)S(1)}, ...), condition=%wide.while_cond.5, body=%wide.while_body.5.sunk | while | flops 262163 | bytes 5243051 | solution.py:71
  38.3 3.6 dynamic-slice_select_fusion.9
  41.9 5.1 dynamic-update-slice.33
  50.3 3.6 dynamic-slice_select_fusion.9
  53.9 5.1 dynamic-update-slice.33
  63.3 32.5 %reduce-scatter.5.cloned.1.call-done = f32[16,2,8,1024]{3,2,1,0:T(8,128)} async-done(((f32[32,2,8,1024]{3,2,1,0:T(8,128)}), f32[16,2,8,1024]{3,2,1,0:T(8,128)}) %reduce-scatter.5.cloned.1.call-update) | async-done | bytes 1048592 | tf_op jit(solution)/shard_map/reduce_scatter | solution.py:24
  96.4 17.8 %fusion.50 = f32[2,8,1024]{2,1,0:T(8,128)S(1)} fusion(f32[2,8,1024]{2,1,0:T(8,128)S(1)} %copy-done), kind=kOutput, calls=%fused_computation.67 | convolution fusion | flops 216006656 | bytes 131072 | tf_op jit(solution)/shard_map/dot_general | solution.py:113
  114.3 18.0 %broadcast_multiply_fusion = (f32[2,8,1024]{2,1,0:T(8,128)S(1)}, f32[2,8,1024]{2,1,0:T(8,128)S(1)}, f32[2,8,1024]{2,1,0:T(8,128)S(1)}, f32[2,8,1024]{2,1,0:T(8,128)S(1)}) fusion(f32[1024]{0:T(1024)S(1)} %get-tuple-element.358, f32[2,1024]{1,0:T(2,128)S(1)} %get-tuple-element.348, f32[2,8,1024]{2,1,0:T(8,128)S(1)} %fusion.50, ...), kind=kOutput, calls=%fused_computation.102 | convolution fusion | flops 216154112 | bytes 417792 | tf_op jit(solution)/shard_map/dot_general | solution.py:114
  132.3 18.4 %fusion.24 = f32[32,1024]{1,0:T(8,128)S(1)} fusion(f32[2,8,1024]{2,1,0:T(8,128)S(1)} %get-tuple-element.345, f32[2,8,1024]{2,1,0:T(8,128)S(1)} %get-tuple-element.324), kind=kOutput, calls=%fused_computation.53 | convolution fusion | flops 417366016 | bytes 262144 | tf_op jit(solution)/shard_map/dot_general | solution.py:121
  150.7 18.0 %fusion.47 = f32[32,1024]{1,0:T(8,128)S(1)} fusion(f32[32,1024]{1,0:T(8,128)S(1)} %fusion.24, f32[2,8,1024]{2,1,0:T(8,128)S(1)} %get-tuple-element.323, f32[2,8,1024]{2,1,0:T(8,128)S(1)} %get-tuple-element.346), kind=kOutput, calls=%fused_computation.66 | convolution fusion | flops 417431552 | bytes 393216 | tf_op jit(solution)/shard_map/dot_general | solution.py:122
  170.0 34.9 %all_gather.20 = bf16[16,2,8,1024]{3,2,1,0:T(8,128)(2,1)} all-gather(bf16[1,2,8,1024]{3,2,1,0:T(8,128)(2,1)S(1)} %fusion.69), channel_id=1, replica_groups=mesh['grp'=2,'slab_0'=16,'slab_1'=2,'ang'=4] {'slab_0'}, dimensions={0}, use_global_device_ids=true | all-gather | bytes 557056 | tf_op jit(solution)/shard_map/all_gather | solution.py:48
  205.3 15.5 %all-gather.5.cloned.1.call-done = bf16[32,2,8,1024]{3,2,1,0:T(8,128)(2,1)} async-done(((bf16[16,2,8,1024]{3,2,1,0:T(8,128)(2,1)}), bf16[32,2,8,1024]{3,2,1,0:T(8,128)(2,1)}) %all-gather.5.cloned.1.call-update) | async-done | bytes 1048592 | tf_op jit(solution)/shard_map/all_gather | solution.py:48
  223.0 4.2 fusion.10
  227.8 3.5 add_convert_fusion.1
  231.3 42.2 %all-reduce.6 = f32[2,256,1024]{2,1,0:T(8,128)S(1)} all-reduce(bf16[2,256,1024]{2,1,0:T(8,128)(2,1)S(1)} %bitcast.233), channel_id=1, replica_groups=mesh['grp'=2,'slab_0'=16,'slab_1'=2,'ang'=4] {'ang'}, use_global_device_ids=true, to_apply=%region_6.7 | all-reduce | flops 524288 | bytes 3145728 | tf_op jit(solution)/shard_map/psum | solution.py:96
  281.5 17.7 %while.14 = (s32[]{:T(128)}, f32[2,264,1024]{2,1,0:T(8,128)S(1)}, s32[2,3]{1,0:T(2,128)S(1)}, f32[2,256,1024]{2,1,0:T(8,128)}, s32[]{:T(128)}, /*index=5*/s32[3]{0:T(128)S(1)}, s32[]{:T(128)}) while((s32[]{:T(128)}, f32[2,264,1024]{2,1,0:T(8,128)S(1)}, s32[2,3]{1,0:T(2,128)S(1)}, f32[2,256,1024]{2,1,0:T(8,128)}, s32[]{:T(128)}, ...), condition=%wide.while_cond.6, body=%wide.while_body.6.sunk | while | flops 262163 | bytes 5243051 | solution.py:71
  293.7 3.3 dynamic-slice_select_fusion.10
  300.7 18.1 %while.15 = (s32[]{:T(128)}, f32[2,264,1024]{2,1,0:T(8,128)S(1)}, s32[2,3]{1,0:T(2,128)S(1)}, f32[2,256,1024]{2,1,0:T(8,128)}, s32[]{:T(128)}, /*index=5*/s32[3]{0:T(128)S(1)}, s32[]{:T(128)}) while((s32[]{:T(128)}, f32[2,264,1024]{2,1,0:T(8,128)S(1)}, s32[2,3]{1,0:T(2,128)S(1)}, f32[2,256,1024]{2,1,0:T(8,128)}, s32[]{:T(128)}, ...), condition=%wide.while_cond.7, body=%wide.while_body.7.sunk | while | flops 262163 | bytes 5243051 | solution.py:71
  304.2 3.4 dynamic-slice_select_fusion.11
  313.2 3.4 dynamic-slice_select_fusion.11
  322.2 20.0 %reduce-scatter.9.cloned.1.call-done = f32[16,2,8,1024]{3,2,1,0:T(8,128)} async-done(((f32[32,2,8,1024]{3,2,1,0:T(8,128)}), f32[16,2,8,1024]{3,2,1,0:T(8,128)}) %reduce-scatter.9.cloned.1.call-update) | async-done | bytes 1048592 | tf_op jit(solution)/shard_map/reduce_scatter | solution.py:24
  342.3 73.3 %reduce-scatter.11.cloned.1.call-done = f32[1,2,8,1024]{3,2,1,0:T(8,128)} async-done(((f32[16,2,8,1024]{3,2,1,0:T(8,128)}), f32[1,2,8,1024]{3,2,1,0:T(8,128)}) %reduce-scatter.11.cloned.1.call-update) | async-done | bytes 65552 | tf_op jit(solution)/shard_map/reduce_scatter | solution.py:24
  416.4 32.8 %all_gather.23 = bf16[16,2,8,1024]{3,2,1,0:T(8,128)(2,1)} all-gather(bf16[1,2,8,1024]{3,2,1,0:T(8,128)(2,1)S(1)} %fusion.70), channel_id=1, replica_groups=mesh['grp'=2,'slab_0'=16,'slab_1'=2,'ang'=4] {'slab_0'}, dimensions={0}, use_global_device_ids=true | all-gather | bytes 557056 | tf_op jit(solution)/shard_map/all_gather | solution.py:48
  451.4 10.5 %all-to-all-start = ((f32[32,1,2]{2,1,0:T(1,128)}), f32[32,1,2]{2,1,0:T(1,128)S(1)}, u32[]{:S(2)}, u32[]{:S(2)}) async-start(f32[32,1,2]{2,1,0:T(1,128)} %broadcast_in_dim.7), calls=%async_computation.4 | async-start | bytes 32768 | tf_op jit(solution)/shard_map/all_to_all | solution.py:61
  461.9 12.1 %all-to-all-done = f32[32,1,2]{2,1,0:T(1,128)S(1)} async-done(((f32[32,1,2]{2,1,0:T(1,128)}), f32[32,1,2]{2,1,0:T(1,128)S(1)}, u32[]{:S(2)}, u32[]{:S(2)}) %all-to-all-start) | async-done | bytes 288 | tf_op jit(solution)/shard_map/all_to_all | solution.py:61
  476.7 4.2 fusion.12
  481.5 4.5 add_convert_fusion
  486.0 42.0 %all-reduce.7 = f32[2,256,1024]{2,1,0:T(8,128)S(1)} all-reduce(bf16[2,256,1024]{2,1,0:T(8,128)(2,1)} %bitcast.234), channel_id=1, replica_groups=mesh['grp'=2,'slab_0'=16,'slab_1'=2,'ang'=4] {'ang'}, use_global_device_ids=true, to_apply=%region_13.14 | all-reduce | flops 524288 | bytes 3145728 | tf_op jit(solution)/shard_map/psum | solution.py:96
  (138 shorter events, 79.4 us)
Async XLA Ops:
  7.2 89.2 %copy-start = (f32[2,8,1024]{2,1,0:T(8,128)S(1)}, f32[2,8,1024]{2,1,0:T(8,128)}, u32[]{:S(2)}) copy-start(f32[2,8,1024]{2,1,0:T(8,128)} %param.8) | copy-start | bytes 196612
  7.2 88.6 %reduce-scatter.5.cloned.1.call-start = ((), (), s32[]{:S(2)}) async-start(), calls=%async_computation.5 | async-start | bytes 3145728 | tf_op jit(solution)/shard_map/reduce_scatter | solution.py:24
  7.3 4.7 copy-start.5
  7.3 4.7 copy-start.10
  12.0 2.6 copy-start.7
  12.0 2.7 copy-start.8
  14.6 0.7 copy-start.6
  63.1 33.1 %copy-start.9 = (f32[2]{0:T(128)S(1)}, f32[2]{0:T(128)}, u32[]{:S(2)}) copy-start(f32[2]{0:T(128)} %param.9) | copy-start | bytes 28
  63.2 106.0 %reduce-scatter.7.cloned.1.call-start = ((), (), s32[]{:S(2)}) async-start(), calls=%async_computation.6 | async-start | bytes 1114112 | tf_op jit(solution)/shard_map/reduce_scatter | solution.py:24
  95.8 124.9 %all-gather.5.cloned.1.call-start = ((), (), s32[]{:S(2)}) async-start(), calls=%async_computation.9 | async-start | bytes 1572864 | tf_op jit(solution)/shard_map/all_gather | solution.py:48
  205.0 137.2 %reduce-scatter.9.cloned.1.call-start = ((), (), s32[]{:S(2)}) async-start(), calls=%async_computation.7 | async-start | bytes 3145728 | tf_op jit(solution)/shard_map/reduce_scatter | solution.py:24
  273.5 2.5 copy-start.11
  276.0 2.6 copy-start.3
  319.0 1.2 copy-start.2
  322.1 93.5 %reduce-scatter.11.cloned.1.call-start = ((), (), s32[]{:S(2)}) async-start(), calls=%async_computation.8 | async-start | bytes 1114112 | tf_op jit(solution)/shard_map/reduce_scatter | solution.py:24
  342.3 132.4 %all-gather.7.cloned.1.call-start = ((), (), s32[]{:S(2)}) async-start(), calls=%async_computation.10 | async-start | bytes 1572864 | tf_op jit(solution)/shard_map/all_gather | solution.py:48
  451.4 22.6 %all-to-all-start = ((f32[32,1,2]{2,1,0:T(1,128)}), f32[32,1,2]{2,1,0:T(1,128)S(1)}, u32[]{:S(2)}, u32[]{:S(2)}) async-start(f32[32,1,2]{2,1,0:T(1,128)} %broadcast_in_dim.7), calls=%async_computation.4 | async-start | bytes 32768 | tf_op jit(solution)/shard_map/all_to_all | solution.py:61
  486.0 42.0 %copy-start.4 = (bf16[2,256,1024]{2,1,0:T(8,128)(2,1)S(1)}, bf16[2,256,1024]{2,1,0:T(8,128)(2,1)}, u32[]{:S(2)}) copy-start(bf16[2,256,1024]{2,1,0:T(8,128)(2,1)} %copy-done.3) | copy-start | bytes 3145732
  486.0 43.4 %copy-start.1 = (f32[2,8,1024]{2,1,0:T(8,128)S(1)}, f32[2,8,1024]{2,1,0:T(8,128)}, u32[]{:S(2)}) copy-start(f32[2,8,1024]{2,1,0:T(8,128)} %param.8) | copy-start | bytes 196612
Sparse Core Ops, SparseCore 0:
  63.3 32.4 reduce-scatter.4
  98.3 70.8 reduce-scatter.6
  205.1 15.5 all-gather.4
  322.2 19.9 reduce-scatter.8
  344.6 70.9 reduce-scatter.10
  449.5 16.1 all-gather.6
where the time goes:
time: 542 us; the launch traced here: 536 us
  waiting for transfers between devices  154 us (28%)
  blocking collectives  152 us (28%)
  matrix products  101 us (19%)
  other arithmetic  59.6 us (11%)
  local copies, waits for them, and re-layouts  43 us (8%)
  between operations  14.8 us (3%)
  starting transfers between devices  11.1 us (2%)
    reduce_scatter x4, waiting for transfers between devices, own_block(): tiles = lax.psum_scatter(tiles, axes[k], scatter_dimension=0, tiled=True)  126 us
    psum x2, blocking collectives, apply_update(): gradient = lax.psum(partial_wide, 'ang')  84.2 us
    all_gather x2, blocking collectives, stacked_from(): tiles = lax.all_gather(tiles, axes[k])  67.7 us
    scatter x16, other arithmetic  49.3 us
    scatter x24, local copies, waits for them, and re-layouts  28.3 us
    dot_general x1, matrix products, per_device(): jnp.dot(first_half, cosine, precision=highest)  18.4 us
    dot_general x1, matrix products, per_device(): jnp.dot(flat_rows, sine, precision=highest)  18 us
    dot_general x1, matrix products, per_device(): jnp.dot(second_half, sine, precision=highest)  18 us
  transfers between devices with their start and end apart: 7, of which 6 were waited for; matrix products, arithmetic and copies ran while one was open for 14% of the time, Pallas kernels for 0%

commit v1 on v0

--- a/solution.py
+++ b/solution.py
@@ -4,6 +4,7 @@
 from jax import lax
 from jax.sharding import Mesh
 from jax.sharding import PartitionSpec as P
+from jax.lax import axis_size, ppermute
 
 Y = 256
 X = 1024
@@ -91,9 +92,20 @@
 
 
 def apply_update(current, running):
+
+    def load_tiles(here_x, shard_axis):
+        size_here = axis_size(shard_axis)
+        tmp = here_x
+        for w in [
+            [(dd, dd ^ t) for dd in range(size_here)] for t in (1, 2, 4, 8, 16) if t < size_here
+        ]:
+            current_arr = ppermute(tmp, axis_name=shard_axis, perm=w)
+            tmp = tmp + current_arr
+        return tmp
+
     partial_value = lax.optimization_barrier(running.reshape(current.shape).astype(jnp.bfloat16))
     partial_wide = partial_value.astype(jnp.float32)
-    gradient = lax.psum(partial_wide, "ang")
+    gradient = load_tiles(partial_wide, "ang")
     renewed = (current.astype(jnp.float32) - step_size * gradient).astype(jnp.bfloat16)
     return renewed
 

time: 542 us -> 644 us (1.19)
  waiting for transfers between devices: 154 us -> 319 us
  blocking collectives: 152 us -> 92.2 us
    ppermute x0 -> x4, waiting for transfers between devices: none -> 160 us  [load_tiles(): current_arr = ppermute(tmp, axis_name=shard_axis, perm=w)]
    psum x2 -> x0, blocking collectives: 84.2 us -> none  [apply_update(): gradient = lax.psum(partial_wide, 'ang')]
    all_to_all x0 -> x1, blocking collectives: none -> 24.7 us  [from_everyone(): return lax.all_to_all(copies, axis, split_axis=0, concat_axis=0, tiled=True)]
    all_gather x2, waiting for transfers between devices: 15.5 us -> 32.3 us  [stacked_from(): tiles = lax.all_gather(tiles, axes[k])]
    all_to_all x1 -> x0, waiting for transfers between devices: 12.1 us -> none  [from_everyone(): return lax.all_to_all(copies, axis, split_axis=0, concat_axis=0, tiled=True)]
    all_to_all x1 -> x0, starting transfers between devices: 10.5 us -> none  [from_everyone(): return lax.all_to_all(copies, axis, split_axis=0, concat_axis=0, tiled=True)]
    ppermute x0 -> x4, starting transfers between devices: none -> 7.18 us  [load_tiles(): current_arr = ppermute(tmp, axis_name=shard_axis, perm=w)]
  transfers between devices with their start and end apart: 7 -> 10, of which waited for: 6 -> 10; matrix products, arithmetic and copies ran while one was open for 14% -> 12% of each run, Pallas kernels for 0% -> 0%
where the time goes in v1:
time: 644 us; the launch traced here: 638 us
  waiting for transfers between devices  319 us (50%)
  matrix products  100 us (16%)
  blocking collectives  92.2 us (14%)
  other arithmetic  62.1 us (10%)
  local copies, waits for them, and re-layouts  41.3 us (6%)
  between operations  14.8 us (2%)
  starting transfers between devices  7.85 us (1%)
    ppermute x4, waiting for transfers between devices, load_tiles(): current_arr = ppermute(tmp, axis_name=shard_axis, perm=w)  160 us
    reduce_scatter x4, waiting for transfers between devices, own_block(): tiles = lax.psum_scatter(tiles, axes[k], scatter_dimension=0, tiled=True)  126 us
    all_gather x2, blocking collectives, stacked_from(): tiles = lax.all_gather(tiles, axes[k])  67.4 us
    scatter x16, other arithmetic  49.3 us
    all_gather x2, waiting for transfers between devices, stacked_from(): tiles = lax.all_gather(tiles, axes[k])  32.3 us
    scatter x24, local copies, waits for them, and re-layouts  27.9 us
    all_to_all x1, blocking collectives, from_everyone(): return lax.all_to_all(copies, axis, split_axis=0, concat_axis=0, tiled=True)  24.7 us
    dot_general x1, matrix products, per_device(): jnp.dot(first_half, cosine, precision=highest)  18.4 us
  transfers between devices with their start and end apart: 10, of which 10 were waited for; matrix products, arithmetic and copies ran while one was open for 12% of the time, Pallas kernels for 0%

profile of v1, /device:TPU:34, one launch (start us, length us, event | category | flops | bytes accessed | tf_op | source)
XLA Modules:
  0.0 638.3 jit_solution(14561922477371433828)
XLA Ops:
  7.3 4.6 fusion.16
  15.2 17.6 %while.12 = (s32[]{:T(128)}, f32[2,264,1024]{2,1,0:T(8,128)S(1)}, s32[2,3]{1,0:T(2,128)S(1)}, f32[2,256,1024]{2,1,0:T(8,128)}, s32[]{:T(128)}, /*index=5*/s32[3]{0:T(128)S(1)}, s32[]{:T(128)}) while((s32[]{:T(128)}, f32[2,264,1024]{2,1,0:T(8,128)S(1)}, s32[2,3]{1,0:T(2,128)S(1)}, f32[2,256,1024]{2,1,0:T(8,128)}, s32[]{:T(128)}, ...), condition=%wide.while_cond.4, body=%wide.while_body.4.sunk | while | flops 262163 | bytes 5243051 | solution.py:72
  18.5 3.4 dynamic-slice_select_fusion.8
  34.5 24.3 %while.13 = (s32[]{:T(128)}, f32[2,264,1024]{2,1,0:T(8,128)}, s32[2,3]{1,0:T(2,128)S(1)}, f32[2,256,1024]{2,1,0:T(8,128)}, s32[]{:T(128)}, /*index=5*/s32[3]{0:T(128)S(1)}, s32[]{:T(128)}) while((s32[]{:T(128)}, f32[2,264,1024]{2,1,0:T(8,128)}, s32[2,3]{1,0:T(2,128)S(1)}, f32[2,256,1024]{2,1,0:T(8,128)}, s32[]{:T(128)}, /*index=5*/s32[3]{0:T(128)S(1)}, ...), condition=%wide.while_cond.5, body=%wide.while_body.5.sunk | while | flops 262163 | bytes 5243051 | solution.py:72
  37.9 3.7 dynamic-slice_select_fusion.9
  41.7 5.0 dynamic-update-slice.33
  50.1 3.7 dynamic-slice_select_fusion.9
  53.8 5.0 dynamic-update-slice.33
  63.1 32.5 %reduce-scatter.5.cloned.1.call-done = f32[16,2,8,1024]{3,2,1,0:T(8,128)} async-done(((f32[32,2,8,1024]{3,2,1,0:T(8,128)}), f32[16,2,8,1024]{3,2,1,0:T(8,128)}) %reduce-scatter.5.cloned.1.call-update) | async-done | bytes 1048592 | tf_op jit(solution)/shard_map/reduce_scatter | solution.py:25
  96.3 17.8 %fusion.50 = f32[2,8,1024]{2,1,0:T(8,128)S(1)} fusion(f32[2,8,1024]{2,1,0:T(8,128)S(1)} %copy-done), kind=kOutput, calls=%fused_computation.67 | convolution fusion | flops 216006656 | bytes 131072 | tf_op jit(solution)/shard_map/dot_general | solution.py:125
  114.1 18.0 %broadcast_multiply_fusion = (f32[2,8,1024]{2,1,0:T(8,128)S(1)}, f32[2,8,1024]{2,1,0:T(8,128)S(1)}, f32[2,8,1024]{2,1,0:T(8,128)S(1)}, f32[2,8,1024]{2,1,0:T(8,128)S(1)}) fusion(f32[1024]{0:T(1024)S(1)} %get-tuple-element.358, f32[2,1024]{1,0:T(2,128)S(1)} %get-tuple-element.348, f32[2,8,1024]{2,1,0:T(8,128)S(1)} %fusion.50, ...), kind=kOutput, calls=%fused_computation.104 | convolution fusion | flops 216154112 | bytes 417792 | tf_op jit(solution)/shard_map/dot_general | solution.py:126
  132.2 18.4 %fusion.24 = f32[32,1024]{1,0:T(8,128)S(1)} fusion(f32[2,8,1024]{2,1,0:T(8,128)S(1)} %get-tuple-element.345, f32[2,8,1024]{2,1,0:T(8,128)S(1)} %get-tuple-element.324), kind=kOutput, calls=%fused_computation.53 | convolution fusion | flops 417366016 | bytes 262144 | tf_op jit(solution)/shard_map/dot_general | solution.py:133
  150.6 18.0 %fusion.47 = f32[32,1024]{1,0:T(8,128)S(1)} fusion(f32[32,1024]{1,0:T(8,128)S(1)} %fusion.24, f32[2,8,1024]{2,1,0:T(8,128)S(1)} %get-tuple-element.323, f32[2,8,1024]{2,1,0:T(8,128)S(1)} %get-tuple-element.346), kind=kOutput, calls=%fused_computation.66 | convolution fusion | flops 417431552 | bytes 393216 | tf_op jit(solution)/shard_map/dot_general | solution.py:134
  170.0 34.8 %all_gather.20 = bf16[16,2,8,1024]{3,2,1,0:T(8,128)(2,1)} all-gather(bf16[1,2,8,1024]{3,2,1,0:T(8,128)(2,1)S(1)} %fusion.69), channel_id=1, replica_groups=mesh['grp'=2,'slab_0'=16,'slab_1'=2,'ang'=4] {'slab_0'}, dimensions={0}, use_global_device_ids=true | all-gather | bytes 557056 | tf_op jit(solution)/shard_map/all_gather | solution.py:49
  205.1 15.5 %all-gather.5.cloned.1.call-done = bf16[32,2,8,1024]{3,2,1,0:T(8,128)(2,1)} async-done(((bf16[16,2,8,1024]{3,2,1,0:T(8,128)(2,1)}), bf16[32,2,8,1024]{3,2,1,0:T(8,128)(2,1)}) %all-gather.5.cloned.1.call-update) | async-done | bytes 1048592 | tf_op jit(solution)/shard_map/all_gather | solution.py:49
  222.9 4.2 fusion.10
  227.6 3.5 add_convert_fusion.1
  232.8 46.6 %collective-permute-done = f32[2,256,1024]{2,1,0:T(8,128)S(1)} collective-permute-done((f32[2,256,1024]{2,1,0:T(8,128)S(1)}, f32[2,256,1024]{2,1,0:T(8,128)S(1)}, u32[]{:S(2)}, u32[]{:S(2)}) %collective-permute-start) | collective-permute-done | bytes 2097184 | tf_op jit(solution)/shard_map/ppermute | solution.py:102
  281.9 46.5 %collective-permute-done.1 = f32[2,256,1024]{2,1,0:T(8,128)} collective-permute-done((f32[2,256,1024]{2,1,0:T(8,128)S(1)}, f32[2,256,1024]{2,1,0:T(8,128)}, u32[]{:S(2)}, u32[]{:S(2)}) %collective-permute-start.1) | collective-permute-done | bytes 2097184 | tf_op jit(solution)/shard_map/ppermute | solution.py:102
  336.0 17.7 %while.14 = (s32[]{:T(128)}, f32[2,264,1024]{2,1,0:T(8,128)S(1)}, s32[2,3]{1,0:T(2,128)S(1)}, f32[2,256,1024]{2,1,0:T(8,128)}, s32[]{:T(128)}, /*index=5*/s32[3]{0:T(128)S(1)}, s32[]{:T(128)}) while((s32[]{:T(128)}, f32[2,264,1024]{2,1,0:T(8,128)S(1)}, s32[2,3]{1,0:T(2,128)S(1)}, f32[2,256,1024]{2,1,0:T(8,128)}, s32[]{:T(128)}, ...), condition=%wide.while_cond.6, body=%wide.while_body.6.sunk | while | flops 262163 | bytes 5243051 | solution.py:72
  339.4 3.4 dynamic-slice_select_fusion.10
  348.3 3.4 dynamic-slice_select_fusion.10
  355.3 17.7 %while.15 = (s32[]{:T(128)}, f32[2,264,1024]{2,1,0:T(8,128)S(1)}, s32[2,3]{1,0:T(2,128)S(1)}, f32[2,256,1024]{2,1,0:T(8,128)}, s32[]{:T(128)}, /*index=5*/s32[3]{0:T(128)S(1)}, s32[]{:T(128)}) while((s32[]{:T(128)}, f32[2,264,1024]{2,1,0:T(8,128)S(1)}, s32[2,3]{1,0:T(2,128)S(1)}, f32[2,256,1024]{2,1,0:T(8,128)}, s32[]{:T(128)}, ...), condition=%wide.while_cond.7, body=%wide.while_body.7.sunk | while | flops 262163 | bytes 5243051 | solution.py:72
  376.3 20.1 %reduce-scatter.9.cloned.1.call-done = f32[16,2,8,1024]{3,2,1,0:T(8,128)} async-done(((f32[32,2,8,1024]{3,2,1,0:T(8,128)}), f32[16,2,8,1024]{3,2,1,0:T(8,128)}) %reduce-scatter.9.cloned.1.call-update) | async-done | bytes 1048592 | tf_op jit(solution)/shard_map/reduce_scatter | solution.py:25
  396.6 73.2 %reduce-scatter.11.cloned.1.call-done = f32[1,2,8,1024]{3,2,1,0:T(8,128)} async-done(((f32[16,2,8,1024]{3,2,1,0:T(8,128)}), f32[1,2,8,1024]{3,2,1,0:T(8,128)}) %reduce-scatter.11.cloned.1.call-update) | async-done | bytes 65552 | tf_op jit(solution)/shard_map/reduce_scatter | solution.py:25
  470.7 32.6 %all_gather.23 = bf16[16,2,8,1024]{3,2,1,0:T(8,128)(2,1)} all-gather(bf16[1,2,8,1024]{3,2,1,0:T(8,128)(2,1)S(1)} %fusion.70), channel_id=1, replica_groups=mesh['grp'=2,'slab_0'=16,'slab_1'=2,'ang'=4] {'slab_0'}, dimensions={0}, use_global_device_ids=true | all-gather | bytes 557056 | tf_op jit(solution)/shard_map/all_gather | solution.py:49
  503.4 16.8 %all-gather.7.cloned.1.call-done = bf16[32,2,8,1024]{3,2,1,0:T(8,128)(2,1)} async-done(((bf16[16,2,8,1024]{3,2,1,0:T(8,128)(2,1)}), bf16[32,2,8,1024]{3,2,1,0:T(8,128)(2,1)}) %all-gather.7.cloned.1.call-update) | async-done | bytes 1048592 | tf_op jit(solution)/shard_map/all_gather | solution.py:49
  522.5 4.2 fusion.12
  527.3 3.5 add_convert_fusion
  532.4 46.6 %collective-permute-done.2 = f32[2,256,1024]{2,1,0:T(8,128)S(1)} collective-permute-done((f32[2,256,1024]{2,1,0:T(8,128)S(1)}, f32[2,256,1024]{2,1,0:T(8,128)S(1)}, u32[]{:S(2)}, u32[]{:S(2)}) %collective-permute-start.2) | collective-permute-done | bytes 2097184 | tf_op jit(solution)/shard_map/ppermute | solution.py:102
  582.2 24.7 %all_to_all.6 = f32[32,1,2]{2,1,0:T(1,128)S(1)} all-to-all(f32[32,1,2]{2,1,0:T(1,128)S(1)} %broadcast_in_dim.7), channel_id=1, replica_groups=mesh['grp'=2,'slab_0'=16,'slab_1'=2,'ang'=4] {'slab_0','slab_1'}, dimensions={0} | all-to-all | bytes 512 | tf_op jit(solution)/shard_map/all_to_all | solution.py:62
  607.5 20.5 %collective-permute-done.3 = f32[2,256,1024]{2,1,0:T(8,128)} collective-permute-done((f32[2,256,1024]{2,1,0:T(8,128)S(1)}, f32[2,256,1024]{2,1,0:T(8,128)}, u32[]{:S(2)}, u32[]{:S(2)}) %collective-permute-start.3) | collective-permute-done | bytes 2097184 | tf_op jit(solution)/shard_map/ppermute | solution.py:102
  (151 shorter events, 94.1 us)
Async XLA Ops:
  7.2 89.1 %copy-start = (f32[2,8,1024]{2,1,0:T(8,128)S(1)}, f32[2,8,1024]{2,1,0:T(8,128)}, u32[]{:S(2)}) copy-start(f32[2,8,1024]{2,1,0:T(8,128)} %param.8) | copy-start | bytes 196612
  7.2 88.4 %reduce-scatter.5.cloned.1.call-start = ((), (), s32[]{:S(2)}) async-start(), calls=%async_computation.5 | async-start | bytes 3145728 | tf_op jit(solution)/shard_map/reduce_scatter | solution.py:25
  7.3 4.7 copy-start.5
  7.3 4.7 copy-start.12
  11.9 2.6 copy-start.9
  11.9 2.7 copy-start.10
  14.5 0.7 copy-start.8
  63.0 33.1 %copy-start.11 = (f32[2]{0:T(128)S(1)}, f32[2]{0:T(128)}, u32[]{:S(2)}) copy-start(f32[2]{0:T(128)} %param.9) | copy-start | bytes 28
  63.1 106.0 %reduce-scatter.7.cloned.1.call-start = ((), (), s32[]{:S(2)}) async-start(), calls=%async_computation.6 | async-start | bytes 1114112 | tf_op jit(solution)/shard_map/reduce_scatter | solution.py:25
  95.7 124.9 %all-gather.5.cloned.1.call-start = ((), (), s32[]{:S(2)}) async-start(), calls=%async_computation.9 | async-start | bytes 1572864 | tf_op jit(solution)/shard_map/all_gather | solution.py:49
  204.8 191.6 %reduce-scatter.9.cloned.1.call-start = ((), (), s32[]{:S(2)}) async-start(), calls=%async_computation.7 | async-start | bytes 3145728 | tf_op jit(solution)/shard_map/reduce_scatter | solution.py:25
  231.4 97.0 %copy-start.6 = (bf16[2,256,1024]{2,1,0:T(8,128)(2,1)S(1)}, bf16[2,256,1024]{2,1,0:T(8,128)(2,1)}, u32[]{:S(2)}) copy-start(bf16[2,256,1024]{2,1,0:T(8,128)(2,1)} %param.5) | copy-start | bytes 3145732
  231.4 47.9 %collective-permute-start = (f32[2,256,1024]{2,1,0:T(8,128)S(1)}, f32[2,256,1024]{2,1,0:T(8,128)S(1)}, u32[]{:S(2)}, u32[]{:S(2)}) collective-permute-start(f32[2,256,1024]{2,1,0:T(8,128)S(1)} %convert_element_type.67), channel_id=1, source_target_pairs={{0,1},{1,0},{2,3},{3,2},{4,5},{5,4},{6,7},{7,6},{8,9},{9,8},{10,11... | collective-permute-start | bytes 6291464 | tf_op jit(solution)/shard_map/ppermute | solution.py:102
  279.7 48.7 %collective-permute-start.1 = (f32[2,256,1024]{2,1,0:T(8,128)S(1)}, f32[2,256,1024]{2,1,0:T(8,128)}, u32[]{:S(2)}, u32[]{:S(2)}) collective-permute-start(f32[2,256,1024]{2,1,0:T(8,128)S(1)} %convert_add_fusion.1), channel_id=1, source_target_pairs={{0,2},{1,3},{2,0},{3,1},{4,6},{5,7},{6,4},{7,5},{8,10},{9,11},{10,... | collective-permute-start | bytes 6291464 | tf_op jit(solution)/shard_map/ppermute | solution.py:102
  281.9 48.7 %copy-start.13 = (bf16[2,1024,1024]{2,1,0:T(8,128)(2,1)S(1)}, bf16[2,1024,1024]{2,1,0:T(8,128)(2,1)}, u32[]{:S(2)}) copy-start(bf16[2,1024,1024]{2,1,0:T(8,128)(2,1)} %param.6) | copy-start | bytes 12582916
  330.6 2.6 copy-start.3
  373.3 1.2 copy-start.2
  376.3 93.6 %reduce-scatter.11.cloned.1.call-start = ((), (), s32[]{:S(2)}) async-start(), calls=%async_computation.8 | async-start | bytes 1114112 | tf_op jit(solution)/shard_map/reduce_scatter | solution.py:25
  396.5 123.7 %all-gather.7.cloned.1.call-start = ((), (), s32[]{:S(2)}) async-start(), calls=%async_computation.10 | async-start | bytes 1572864 | tf_op jit(solution)/shard_map/all_gather | solution.py:49
  531.0 50.5 %copy-start.7 = (f32[1,2,8,1024]{3,2,1,0:T(8,128)S(1)}, f32[1,2,8,1024]{3,2,1,0:T(8,128)}, u32[]{:S(2)}) copy-start(f32[1,2,8,1024]{3,2,1,0:T(8,128)} %reduce-scatter.11.cloned.1.call-done) | copy-start | bytes 196612
  531.0 97.0 %copy-start.4 = (bf16[2,256,1024]{2,1,0:T(8,128)(2,1)S(1)}, bf16[2,256,1024]{2,1,0:T(8,128)(2,1)}, u32[]{:S(2)}) copy-start(bf16[2,256,1024]{2,1,0:T(8,128)(2,1)} %copy-done.3) | copy-start | bytes 3145732
  531.0 48.0 %collective-permute-start.2 = (f32[2,256,1024]{2,1,0:T(8,128)S(1)}, f32[2,256,1024]{2,1,0:T(8,128)S(1)}, u32[]{:S(2)}, u32[]{:S(2)}) collective-permute-start(f32[2,256,1024]{2,1,0:T(8,128)S(1)} %convert_element_type.73), channel_id=1, source_target_pairs={{0,1},{1,0},{2,3},{3,2},{4,5},{5,4},{6,7},{7,6},{8,9},{9,8},{10,11... | collective-permute-start | bytes 6291464 | tf_op jit(solution)/shard_map/ppermute | solution.py:102
  579.3 48.7 %collective-permute-start.3 = (f32[2,256,1024]{2,1,0:T(8,128)S(1)}, f32[2,256,1024]{2,1,0:T(8,128)}, u32[]{:S(2)}, u32[]{:S(2)}) collective-permute-start(f32[2,256,1024]{2,1,0:T(8,128)S(1)} %convert_add_fusion), channel_id=1, source_target_pairs={{0,2},{1,3},{2,0},{3,1},{4,6},{5,7},{6,4},{7,5},{8,10},{9,11},{10,... | collective-permute-start | bytes 6291464 | tf_op jit(solution)/shard_map/ppermute | solution.py:102
  607.0 24.2 %copy-start.1 = (f32[2,8,1024]{2,1,0:T(8,128)S(1)}, f32[2,8,1024]{2,1,0:T(8,128)}, u32[]{:S(2)}) copy-start(f32[2,8,1024]{2,1,0:T(8,128)} %param.8) | copy-start | bytes 196612
Sparse Core Ops, SparseCore 0:
  63.2 32.4 reduce-scatter.4
  98.2 70.8 reduce-scatter.6
  205.0 15.6 all-gather.4
  376.4 20.0 reduce-scatter.8
  398.9 70.9 reduce-scatter.10
  503.5 16.6 all-gather.6
